TPU v7x, 32 devices: a whole 2x2x4 slice. The times are simulated.
32 devices in a mesh: row: 4 (over x, core), col: 8 (over z, y).
Axes of the slice: x: 2, y: 2, z: 4, core: 2. Of those that a mesh axis runs over, the one named last changes fastest.
Arguments:
- matrix: float32 [3072, 12, 4096], P('row', None, 'col'), may hold values from -6 to 6
- factor: float32 [12, 4096, 2048], P(None, 'col', 'row'), as said below
Outputs:
- updated: float32 [3072, 12, 4096], P('row', None, 'col')
- solved: float32 [3072, 2048], P('row')
Inputs may be any that keep to these rules, and one draw needn't show every extreme that they name: factor is lower trapezoidal: zero wherever the column index exceeds the row index; its diagonal entries lie in 1 to 2.
All inputs are finite; a program needn't handle non-finite values.
Results may differ from a plain program's by a relative error of at most 0.00013.
Values sent between devices are 32-bit elements; how exact they have to be, the bound alone decides.
A program may use at most 256 MiB of HBM per device.

v0:
```python
import jax
import jax.numpy as jnp
from jax import lax
from jax.sharding import PartitionSpec as P

P_SIZE = 4


def from_root(value, axis, source):
    kept = jnp.where(lax.axis_index(axis) == source, value, 0).astype(value.dtype)
    return lax.psum(kept, axis)


def local(matrix, factor):
    col_count = lax.axis_size("col")
    col_index = lax.axis_index("col")
    nlocal = matrix.shape[1]
    block_width = matrix.shape[2]
    block_ids = jnp.arange(nlocal, dtype=jnp.int32) * col_count + col_index
    unit_block = jnp.eye(block_width, dtype=jnp.float32)
    panels = []
    columns = lax.all_gather(factor, "row", axis=2, tiled=True)
    current = matrix
    for step in range(P_SIZE):
        local_block = step // col_count
        part_cols = columns[:, :, step * block_width : (step + 1) * block_width]
        root_col = step % col_count
        guarded = jnp.where(col_index == root_col, part_cols[local_block], unit_block)
        solved_block = lax.linalg.triangular_solve(
            guarded, current[:, local_block, :], left_side=False, lower=True, transpose_a=True
        )
        solved_block = from_root(solved_block, "col", root_col)
        panels.append(solved_block)
        product_term = jnp.einsum(
            "ms,lts->mlt", solved_block, part_cols, precision=lax.Precision.HIGHEST
        )
        later_block = (block_ids > step)[None, :, None]
        current = jnp.where(later_block, current - product_term, current)
    solved = jnp.concatenate(panels, axis=1)
    return (current, solved)


def solution(mesh):
    return jax.shard_map(
        local,
        mesh=mesh,
        in_specs=(P("row", None, "col"), P(None, "col", "row")),
        out_specs=(P("row", None, "col"), P("row", None)),
        check_vma=False,
    )
```

profile of v0, /device:TPU:0, one launch (start us, length us, event | category | flops | bytes accessed | tf_op | source)
XLA Modules:
  0.0 1054.0 jit_solution(15892614803361657785)
XLA Ops:
  9.5 299.9 %all-gather.2.cloned.1.call-done = f32[12,512,2048]{2,1,0:T(8,128)} async-done(((f32[12,512,512]{2,1,0:T(8,128)}), f32[12,512,2048]{2,1,0:T(8,128)}) %all-gather.2.cloned.1.call-update) | async-done | bytes 50331664 | tf_op jit(solution)/shard_map/all_gather | solution.py:22
  309.4 4.2 fusion.43
  313.6 11.5 %while.8 = (s32[]{:T(128)}, f32[512,512]{1,0:T(8,128)}, s32[4,2]{0,1:T(2,128)S(1)}, f32[4,128,128]{2,1,0:T(8,128)S(1)}, s32[]{:T(128)}) while((s32[]{:T(128)}, f32[512,512]{1,0:T(8,128)}, s32[4,2]{0,1:T(2,128)S(1)}, f32[4,128,128]{2,1,0:T(8,128)S(1)}, s32[]{:T(128)}) %tuple.71), condition=%wide.while_cond, body=%wide.while_body.sunk | while | flops 2 | bytes 131189 | solution.py:29
  325.1 39.3 %custom-call.6 = f32[4,128,128]{1,2,0:T(8,128)S(1)} custom-call(f32[4,128,128]{2,1,0:T(8,128)S(1)} %get-tuple-element.29), custom_call_target="InvertDiagBlocksLowerTriangular" | custom-call | tf_op jit(solution)/shard_map/triangular_solve/custom-call.1 | solution.py:29
  370.0 3.1 convolution_subtract_fusion.6
  374.9 11.5 %while.9 = (s32[]{:T(128)}, f32[512,512]{1,0:T(8,128)}, s32[4,2]{0,1:T(2,128)S(1)}, f32[4,128,128]{2,1,0:T(8,128)S(1)}, s32[]{:T(128)}) while((s32[]{:T(128)}, f32[512,512]{1,0:T(8,128)}, s32[4,2]{0,1:T(2,128)S(1)}, f32[4,128,128]{2,1,0:T(8,128)S(1)}, s32[]{:T(128)}) %tuple.93), condition=%wide.while_cond.clone, body=%wide.while_body.clone.sunk | while | flops 2 | bytes 131189 | solution.py:29
  386.5 39.3 %custom-call.7 = f32[4,128,128]{1,2,0:T(8,128)S(1)} custom-call(f32[4,128,128]{2,1,0:T(8,128)S(1)} %get-tuple-element.30), custom_call_target="InvertDiagBlocksLowerTriangular" | custom-call | tf_op jit(solution)/shard_map/triangular_solve/custom-call.1 | solution.py:29
  425.8 38.7 %all-reduce.5.cloned.1.call-done = f32[768,512]{0,1:T(8,128)} async-done(((f32[768,512]{0,1:T(8,128)}), f32[768,512]{0,1:T(8,128)}) %all-reduce.5.cloned.1.call-update) | async-done | bytes 1572880 | tf_op jit(solution)/shard_map/psum | solution.py:11
  464.5 68.7 %subtract_select_fusion.3 = f32[768,12,512]{2,0,1:T(8,128)S(1)} fusion(f32[768,12,512]{2,0,1:T(8,128)} %param.4, pred[12]{0:T(512)(128)(4,1)S(1)} %broadcast_compare_fusion, f32[12,512,2048]{2,1,0:T(8,128)} %all-gather.2.cloned.1.call-done, f32[768,512]{0,1:T(8,128)} %all-reduce.5.cloned.1.call-done), kind=kOutput, calls=%fused_computation.11 | convolution fusion | flops 29000466432 | bytes 51904524 | tf_op jit(solution)/shard_map/ms,lts->mlt/dot_general | solution.py:34
  539.1 3.3 convolution_subtract_fusion.4
  544.3 11.9 %while.10 = (s32[]{:T(128)}, f32[512,512]{1,0:T(8,128)}, s32[4,2]{0,1:T(2,128)S(1)}, f32[4,128,128]{2,1,0:T(8,128)S(1)}, s32[]{:T(128)}) while((s32[]{:T(128)}, f32[512,512]{1,0:T(8,128)}, s32[4,2]{0,1:T(2,128)S(1)}, f32[4,128,128]{2,1,0:T(8,128)S(1)}, s32[]{:T(128)}) %tuple.94), condition=%wide.while_cond.clone.1, body=%wide.while_body.clone.1.sunk | while | flops 2 | bytes 131189 | solution.py:29
  556.2 39.3 %custom-call.8 = f32[4,128,128]{1,2,0:T(8,128)S(1)} custom-call(f32[4,128,128]{2,1,0:T(8,128)S(1)} %get-tuple-element.31), custom_call_target="InvertDiagBlocksLowerTriangular" | custom-call | tf_op jit(solution)/shard_map/triangular_solve/custom-call.1 | solution.py:29
  595.5 37.6 %all-reduce.7.cloned.1.call-done = f32[768,512]{0,1:T(8,128)} async-done(((f32[768,512]{0,1:T(8,128)}), f32[768,512]{0,1:T(8,128)}) %all-reduce.7.cloned.1.call-update) | async-done | bytes 1572880 | tf_op jit(solution)/shard_map/psum | solution.py:11
  633.1 68.9 %subtract_select_fusion.2 = f32[768,12,512]{2,0,1:T(8,128)S(1)} fusion(f32[768,12,512]{2,0,1:T(8,128)} %copy-done.1, pred[12]{0:T(512)(128)(4,1)S(1)} %broadcast_compare_fusion.1, f32[12,512,2048]{2,1,0:T(8,128)} %all-gather.2.cloned.1.call-done, f32[768,512]{0,1:T(8,128)} %all-reduce.7.cloned.1.call-done), kind=kOutput, calls=%fused_computation.10 | convolution fusion | flops 29000466432 | bytes 51904524 | tf_op jit(solution)/shard_map/ms,lts->mlt/dot_general | solution.py:34
  705.0 2.5 convolution_subtract_fusion.9
  708.0 3.3 convolution_subtract_fusion.2
  713.2 8.2 while.11
  721.4 39.3 %custom-call.9 = f32[4,128,128]{1,2,0:T(8,128)S(1)} custom-call(f32[4,128,128]{2,1,0:T(8,128)S(1)} %get-tuple-element.32), custom_call_target="InvertDiagBlocksLowerTriangular" | custom-call | tf_op jit(solution)/shard_map/triangular_solve/custom-call.1 | solution.py:29
  760.7 41.0 %all-reduce.9.cloned.1.call-done = f32[768,512]{0,1:T(8,128)} async-done(((f32[768,512]{0,1:T(8,128)}), f32[768,512]{0,1:T(8,128)}) %all-reduce.9.cloned.1.call-update) | async-done | bytes 1572880 | tf_op jit(solution)/shard_map/psum | solution.py:11
  801.7 68.9 %subtract_select_fusion.1 = f32[768,12,512]{2,0,1:T(8,128)S(1)} fusion(f32[768,12,512]{2,0,1:T(8,128)} %copy-done, pred[12]{0:T(512)(128)(4,1)S(1)} %broadcast_compare_fusion.2, f32[12,512,2048]{2,1,0:T(8,128)} %all-gather.2.cloned.1.call-done, f32[768,512]{0,1:T(8,128)} %all-reduce.9.cloned.1.call-done), kind=kOutput, calls=%fused_computation.9 | convolution fusion | flops 29000466432 | bytes 51904524 | tf_op jit(solution)/shard_map/ms,lts->mlt/dot_general | solution.py:34
  879.3 88.6 %all-reduce.11.cloned.1.call-done = f32[768,512]{0,1:T(8,128)} async-done(((f32[768,512]{0,1:T(8,128)}), f32[768,512]{0,1:T(8,128)}) %all-reduce.11.cloned.1.call-update) | async-done | bytes 1572880 | tf_op jit(solution)/shard_map/psum | solution.py:11
  967.9 5.0 pad_maximum_fusion
  973.0 6.7 copy.8
  979.6 67.6 %subtract_select_fusion = f32[768,12,512]{2,0,1:T(8,128)} fusion(f32[768,12,512]{2,0,1:T(8,128)} %copy-done.2, pred[12]{0:T(512)(128)(4,1)S(1)} %broadcast_compare_fusion.3, f32[12,512,2048]{2,1,0:T(8,128)} %all-gather.2.cloned.1.call-done, f32[768,512]{0,1:T(8,128)S(1)} %copy-done.5), kind=kOutput, calls=%fused_computation.8 | convolution fusion | flops 29000466432 | bytes 51904524 | tf_op jit(solution)/shard_map/ms,lts->mlt/dot_general | solution.py:34
  (112 shorter events, 74.1 us)
Async XLA Ops:
  7.2 302.2 %all-gather.2.cloned.1.call-start = ((), (), s32[]{:S(2)}) async-start(), calls=%async_computation | async-start | bytes 62914560 | tf_op jit(solution)/shard_map/all_gather | solution.py:22
  7.9 456.6 %all-reduce.5.cloned.1.call-start = ((), (), s32[]{:S(2)}) async-start(), calls=%async_computation.1 | async-start | bytes 3145728 | tf_op jit(solution)/shard_map/psum | solution.py:11
  374.8 258.3 %all-reduce.7.cloned.1.call-start = ((), (), s32[]{:S(2)}) async-start(), calls=%async_computation.2 | async-start | bytes 3145728 | tf_op jit(solution)/shard_map/psum | solution.py:11
  533.2 9.2 copy-start.1
  544.2 257.5 %all-reduce.9.cloned.1.call-start = ((), (), s32[]{:S(2)}) async-start(), calls=%async_computation.3 | async-start | bytes 3145728 | tf_op jit(solution)/shard_map/psum | solution.py:11
  702.0 9.2 copy-start
  713.1 254.9 %all-reduce.11.cloned.1.call-start = ((), (), s32[]{:S(2)}) async-start(), calls=%async_computation.4 | async-start | bytes 3145728 | tf_op jit(solution)/shard_map/psum | solution.py:11
  870.7 6.9 copy-start.2
  878.0 89.9 %copy-start.4 = (f32[768,512]{0,1:T(8,128)S(1)}, f32[768,512]{0,1:T(8,128)}, u32[]{:S(2)}) copy-start(f32[768,512]{0,1:T(8,128)} %all-reduce.7.cloned.1.call-done) | copy-start | bytes 4718596
  879.3 88.7 %copy-start.3 = (f32[768,512]{0,1:T(8,128)S(1)}, f32[768,512]{0,1:T(8,128)}, u32[]{:S(2)}) copy-start(f32[768,512]{0,1:T(8,128)} %all-reduce.5.cloned.1.call-done) | copy-start | bytes 4718596
  973.0 6.7 copy-start.5
Sparse Core Ops, SparseCore 0:
  9.5 299.8 all-gather.1
  374.9 89.4 all-reduce.4
  544.3 88.7 all-reduce.6
  713.2 88.5 all-reduce.8
  879.4 88.4 all-reduce.10
where the time goes:
time: 1060 us; the launch traced here: 1050 us
  waiting for transfers between devices  507 us (48%)
  matrix products  309 us (29%)
  other arithmetic  171 us (16%)
  local copies, waits for them, and re-layouts  52.2 us (5%)
  between operations  14.4 us (1%)
    all_gather x1, waiting for transfers between devices, local(): columns = lax.all_gather(factor, 'row', axis=2, tiled=True)  300 us
    dot_general x4, matrix products, local(): jnp.einsum('ms,lts->mlt', solved_block, part_cols, precision=lax.Precisio...  274 us
    psum x4, waiting for transfers between devices, from_root(): return lax.psum(kept, axis)  206 us
    another operation x6, other arithmetic, local(): lax.linalg.triangular_solve(guarded, current[:, local_block, :], left_sid...  161 us
    another operation x53, local copies, waits for them, and re-layouts, local(): lax.linalg.triangular_solve(guarded, current[:, local_block, :], left_sid...  42.9 us
    another operation x28, matrix products, local(): lax.linalg.triangular_solve(guarded, current[:, local_block, :], left_sid...  34.7 us
  transfers between devices with their start and end apart: 5, of which 5 were waited for; matrix products, arithmetic and copies ran while one was open for 14% of the time, Pallas kernels for 0%

commit v1 on v0

--- a/solution.py
+++ b/solution.py
@@ -8,7 +8,8 @@
 
 def from_root(value, axis, source):
     kept = jnp.where(lax.axis_index(axis) == source, value, 0).astype(value.dtype)
-    return lax.psum(kept, axis)
+    lift_the_shelves = lambda vector, mesh_ax: jnp.sum(jax.lax.all_gather(vector, mesh_ax), axis=0)
+    return lift_the_shelves(kept, axis)
 
 
 def local(matrix, factor):

time: 1060 us -> 1500 us (1.42)
  waiting for transfers between devices: 507 us -> 851 us
  local copies, waits for them, and re-layouts: 52.2 us -> 111 us
  other arithmetic: 171 us -> 203 us
    all_gather x0 -> x4, waiting for transfers between devices: none -> 550 us  [from_root(): jax.lax.all_gather(vector, mesh_ax)]
    psum x4 -> x0, waiting for transfers between devices: 206 us -> none  [from_root(): return lax.psum(kept, axis)]
    unnamed x13 -> x21, local copies, waits for them, and re-layouts: 7.45 us -> 67.7 us
    reduce_sum x0 -> x4, other arithmetic: none -> 31.9 us  [from_root(): jnp.sum(jax.lax.all_gather(vector, mesh_ax), axis=0)]
  transfers between devices with their start and end apart: 5 -> 5, of which waited for: 5 -> 5; matrix products, arithmetic and copies ran while one was open for 14% -> 10% of each run, Pallas kernels for 0% -> 0%
where the time goes in v1:
time: 1500 us; the launch traced here: 1490 us
  waiting for transfers between devices  851 us (57%)
  matrix products  315 us (21%)
  other arithmetic  203 us (14%)
  local copies, waits for them, and re-layouts  111 us (7%)
    all_gather x4, waiting for transfers between devices, from_root(): jax.lax.all_gather(vector, mesh_ax)  550 us
    all_gather x1, waiting for transfers between devices, local(): columns = lax.all_gather(factor, 'row', axis=2, tiled=True)  300 us
    dot_general x4, matrix products, local(): jnp.einsum('ms,lts->mlt', solved_block, part_cols, precision=lax.Precisio...  277 us
    another operation x6, other arithmetic, local(): lax.linalg.triangular_solve(guarded, current[:, local_block, :], left_sid...  162 us
    unnamed x21, local copies, waits for them, and re-layouts  67.7 us
    another operation x53, local copies, waits for them, and re-layouts, local(): lax.linalg.triangular_solve(guarded, current[:, local_block, :], left_sid...  41.5 us
    another operation x28, matrix products, local(): lax.linalg.triangular_solve(guarded, current[:, local_block, :], left_sid...  37.6 us
    reduce_sum x4, other arithmetic, from_root(): jnp.sum(jax.lax.all_gather(vector, mesh_ax), axis=0)  31.9 us
  transfers between devices with their start and end apart: 5, of which 5 were waited for; matrix products, arithmetic and copies ran while one was open for 10% of the time, Pallas kernels for 0%

profile of v1, /device:TPU:0, one launch (start us, length us, event | category | flops | bytes accessed | tf_op | source)
XLA Modules:
  0.0 1494.9 jit_solution(8317419061509424902)
XLA Ops:
  9.5 299.9 %all-gather.10.cloned.1.call-done = f32[12,512,2048]{2,1,0:T(8,128)} async-done(((f32[12,512,512]{2,1,0:T(8,128)}), f32[12,512,2048]{2,1,0:T(8,128)}) %all-gather.10.cloned.1.call-update) | async-done | bytes 50331664 | tf_op jit(solution)/shard_map/all_gather | solution.py:23
  313.6 11.3 while.8
  324.9 39.3 %custom-call.6 = f32[4,128,128]{1,2,0:T(8,128)S(1)} custom-call(f32[4,128,128]{2,1,0:T(8,128)S(1)} %get-tuple-element.29), custom_call_target="InvertDiagBlocksLowerTriangular" | custom-call | tf_op jit(solution)/shard_map/triangular_solve/custom-call.1 | solution.py:30
  374.9 11.4 while.9
  386.3 39.3 %custom-call.7 = f32[4,128,128]{1,2,0:T(8,128)S(1)} custom-call(f32[4,128,128]{2,1,0:T(8,128)S(1)} %get-tuple-element.30), custom_call_target="InvertDiagBlocksLowerTriangular" | custom-call | tf_op jit(solution)/shard_map/triangular_solve/custom-call.1 | solution.py:30
  425.6 125.3 %all-gather.12.cloned.1.call-done = f32[6144,512]{0,1:T(8,128)} async-done(((f32[768,512]{0,1:T(8,128)}), f32[6144,512]{0,1:T(8,128)}) %all-gather.12.cloned.1.call-update) | async-done | bytes 12582928 | tf_op jit(solution)/shard_map/all_gather | solution.py:11
  550.9 15.2 %copy.17 = f32[64,8,8,768]{3,2,1,0:T(8,128)} copy(f32[64,8,8,768]{3,1,2,0:T(8,128)} %bitcast.165) | data formatting | bytes 25165824
  566.1 7.6 bitcast_reduce_fusion.3
  573.7 69.4 %subtract_select_fusion.3 = f32[768,12,512]{2,0,1:T(8,128)S(1)} fusion(f32[768,12,512]{2,0,1:T(8,128)} %param.4, pred[12]{0:T(512)(128)(4,1)S(1)} %broadcast_compare_fusion, f32[12,512,2048]{2,1,0:T(8,128)} %all-gather.10.cloned.1.call-done, f32[768,512]{0,1:T(8,128)S(1)} %bitcast_reduce_fusion.3), kind=kOutput, calls=%fused_computation.11 | convolution fusion | flops 29000466432 | bytes 51904524 | tf_op jit(solution)/shard_map/ms,lts->mlt/dot_general | solution.py:35
  654.2 7.7 while.10
  662.0 39.3 %custom-call.8 = f32[4,128,128]{1,2,0:T(8,128)S(1)} custom-call(f32[4,128,128]{2,1,0:T(8,128)S(1)} %get-tuple-element.31), custom_call_target="InvertDiagBlocksLowerTriangular" | custom-call | tf_op jit(solution)/shard_map/triangular_solve/custom-call.1 | solution.py:30
  701.3 127.3 %all-gather.14.cloned.1.call-done = f32[6144,512]{0,1:T(8,128)} async-done(((f32[768,512]{0,1:T(8,128)}), f32[6144,512]{0,1:T(8,128)}) %all-gather.14.cloned.1.call-update) | async-done | bytes 12582928 | tf_op jit(solution)/shard_map/all_gather | solution.py:11
  828.6 14.9 copy.18
  851.1 69.4 %subtract_select_fusion.2 = f32[768,12,512]{2,0,1:T(8,128)S(1)} fusion(f32[768,12,512]{2,0,1:T(8,128)} %copy-done.1, pred[12]{0:T(512)(128)(4,1)S(1)} %broadcast_compare_fusion.1, f32[12,512,2048]{2,1,0:T(8,128)} %all-gather.10.cloned.1.call-done, f32[768,512]{0,1:T(8,128)S(1)} %bitcast_reduce_fusion.2), kind=kOutput, calls=%fused_computation.10 | convolution fusion | flops 29000466432 | bytes 51904524 | tf_op jit(solution)/shard_map/ms,lts->mlt/dot_general | solution.py:35
  931.6 11.4 while.11
  942.9 39.9 %custom-call.9 = f32[4,128,128]{1,2,0:T(8,128)} custom-call(f32[4,128,128]{2,1,0:T(8,128)S(1)} %get-tuple-element.32), custom_call_target="InvertDiagBlocksLowerTriangular" | custom-call | tf_op jit(solution)/shard_map/triangular_solve/custom-call.1 | solution.py:30
  982.9 123.1 %all-gather.16.cloned.1.call-done = f32[6144,512]{0,1:T(8,128)} async-done(((f32[768,512]{0,1:T(8,128)}), f32[6144,512]{0,1:T(8,128)}) %all-gather.16.cloned.1.call-update) | async-done | bytes 12582928 | tf_op jit(solution)/shard_map/all_gather | solution.py:11
  1105.9 14.9 copy.19
  1120.8 7.9 bitcast_reduce_fusion.1
  1128.8 70.9 %subtract_select_fusion.1 = f32[768,12,512]{2,0,1:T(8,128)S(1)} fusion(f32[768,12,512]{2,0,1:T(8,128)} %copy-done, pred[12]{0:T(512)(128)(4,1)S(1)} %broadcast_compare_fusion.2, f32[12,512,2048]{2,1,0:T(8,128)} %all-gather.10.cloned.1.call-done, f32[768,512]{0,1:T(8,128)S(1)} %bitcast_reduce_fusion.1), kind=kOutput, calls=%fused_computation.9 | convolution fusion | flops 29000466432 | bytes 51904524 | tf_op jit(solution)/shard_map/ms,lts->mlt/dot_general | solution.py:35
  1211.5 174.4 %all-gather.18.cloned.1.call-done = f32[6144,512]{0,1:T(8,128)} async-done(((f32[768,512]{0,1:T(8,128)}), f32[6144,512]{0,1:T(8,128)}) %all-gather.18.cloned.1.call-update) | async-done | bytes 12582928 | tf_op jit(solution)/shard_map/all_gather | solution.py:11
  1385.9 15.1 %copy.20 = f32[64,8,8,768]{3,2,1,0:T(8,128)} copy(f32[64,8,8,768]{3,1,2,0:T(8,128)} %bitcast.167) | data formatting | bytes 25165824
  1401.0 8.8 bitcast_reduce_fusion
  1420.6 67.4 %subtract_select_fusion = f32[768,12,512]{2,0,1:T(8,128)} fusion(f32[768,12,512]{2,0,1:T(8,128)} %copy-done.2, pred[12]{0:T(512)(128)(4,1)S(1)} %broadcast_compare_fusion.3, f32[12,512,2048]{2,1,0:T(8,128)} %all-gather.10.cloned.1.call-done, f32[768,512]{0,1:T(8,128)S(1)} %copy-done.5), kind=kOutput, calls=%fused_computation.8 | convolution fusion | flops 29000466432 | bytes 51904524 | tf_op jit(solution)/shard_map/ms,lts->mlt/dot_general | solution.py:35
  (124 shorter events, 110.7 us)
Async XLA Ops:
  7.2 302.2 %all-gather.10.cloned.1.call-start = ((), (), s32[]{:S(2)}) async-start(), calls=%async_computation | async-start | bytes 62914560 | tf_op jit(solution)/shard_map/all_gather | solution.py:23
  7.9 543.0 %all-gather.12.cloned.1.call-start = ((), (), s32[]{:S(2)}) async-start(), calls=%async_computation.1 | async-start | bytes 14155776 | tf_op jit(solution)/shard_map/all_gather | solution.py:11
  374.7 453.9 %all-gather.14.cloned.1.call-start = ((), (), s32[]{:S(2)}) async-start(), calls=%async_computation.2 | async-start | bytes 14155776 | tf_op jit(solution)/shard_map/all_gather | solution.py:11
  643.1 9.2 copy-start.1
  654.1 451.8 %all-gather.16.cloned.1.call-start = ((), (), s32[]{:S(2)}) async-start(), calls=%async_computation.3 | async-start | bytes 14155776 | tf_op jit(solution)/shard_map/all_gather | solution.py:11
  662.0 166.7 %copy-start.6 = (f32[512,512]{1,0:T(8,128)}, f32[512,512]{1,0:T(8,128)S(1)}, u32[]{:S(2)}) copy-start(f32[512,512]{1,0:T(8,128)S(1)} %get-tuple-element.276) | copy-start | bytes 3145732
  920.4 9.2 copy-start
  931.5 454.4 %all-gather.18.cloned.1.call-start = ((), (), s32[]{:S(2)}) async-start(), calls=%async_computation.4 | async-start | bytes 14155776 | tf_op jit(solution)/shard_map/all_gather | solution.py:11
  1128.7 70.9 %copy-start.3 = (f32[768,512]{0,1:T(8,128)}, f32[768,512]{0,1:T(8,128)S(1)}, u32[]{:S(2)}) copy-start(f32[768,512]{0,1:T(8,128)S(1)} %bitcast_reduce_fusion.1) | copy-start | bytes 4718596
  1199.6 10.0 copy-start.2
  1199.6 1.1 copy-start.7
  1401.0 8.8 copy-start.4
  1413.9 6.7 copy-start.5
Sparse Core Ops, SparseCore 0:
  9.5 299.8 all-gather.9
  374.8 176.0 all-gather.11
  654.2 174.3 all-gather.13
  931.6 174.2 all-gather.15
  1211.6 174.2 all-gather.17
